TPU v7x, 32 devices: a whole 2x2x4 slice. The times are simulated.
32 devices in a mesh: ha: 4 (over y, x), wa: 8 (over z, core).
Axes of the slice: x: 2, y: 2, z: 4, core: 2. Of those that a mesh axis runs over, the one named last changes fastest.
Arguments:
- tokens: bfloat16 [112, 224, 384], P('ha', 'wa'), may hold values from -8 to 8
- cotangent: bfloat16 [112, 224, 384], P('ha', 'wa'), may hold values from -8 to 8
- w_qkv: bfloat16 [384, 1152], replicated, may hold values from -0.3125 to 0.3125
- w_proj: bfloat16 [384, 384], replicated, may hold values from -0.3125 to 0.3125
- w_fc1: bfloat16 [384, 1536], replicated, may hold values from -0.3125 to 0.3125
- w_fc2: bfloat16 [1536, 384], replicated, may hold values from -0.15625 to 0.15625
- bias_table: float32 [169, 12], replicated, may hold values from -4 to 280
- rel_index: int32 [49, 49], replicated, may hold values from 0 to 168, as said below
- region: int32 [112, 224], P('ha', 'wa'), may hold values from 0 to 15, as said below
Outputs:
- block_out: bfloat16 [112, 224, 384], P('ha', 'wa')
- token_grad: bfloat16 [112, 224, 384], P('ha', 'wa')
- grad_qkv: float32 [384, 1152], replicated
- grad_proj: float32 [384, 384], replicated
- grad_fc1: float32 [384, 1536], replicated
- grad_fc2: float32 [1536, 384], replicated
- grad_table: float32 [169, 12], replicated
Inputs may be any that keep to these rules, and one draw needn't show every extreme that they name: `rel_index`: pairs of window positions with the same offset share an entry, pairs with different offsets have different entries. `region`: the crop id of the token at each position of the shifted grid.
All inputs are finite; a program needn't handle non-finite values.
Results may differ from a plain program's by a relative error of at most 0.016.
Values may be sent and summed in bfloat16 or wider, within the bound.
A program may use at most 128 MiB of HBM per device.

v0:
```python
import math

import jax
import jax.numpy as jnp
from jax import lax
from jax.sharding import PartitionSpec as P

HEADS = 12
SIDE = 7
SHIFT = 3
HEAD_DIM = 32
WINDOW = 49
TABLE = 169
PARAMS = 1771500


epsilon = 1e-05
highest = lax.Precision.HIGHEST


def from_behind(x, axis, by):
    count = lax.axis_size(axis)
    return lax.ppermute(x, axis, [(i, (i + by) % count) for i in range(count)])


def normalize(values):
    average = jnp.mean(values, -1, keepdims=True)
    centred = values - average
    inverse = lax.rsqrt(jnp.mean(centred * centred, -1, keepdims=True) + epsilon)
    return (centred * inverse, inverse)


def normalize_back(normal_rows, inverse, upstream):
    up_mean = jnp.mean(upstream, -1, keepdims=True)
    cross_mean = jnp.mean(upstream * normal_rows, -1, keepdims=True)
    return inverse * (upstream - up_mean - normal_rows * cross_mean)


def gelu_slope(pre_act):
    normal_cdf = 0.5 * (1.0 + lax.erf(pre_act * 2.0 ** (-0.5)))
    return normal_cdf + pre_act * jnp.exp(-0.5 * pre_act * pre_act) * (2.0 * math.pi) ** (-0.5)


def contract(left_in, right_in):
    return lax.dot_general(
        left_in, right_in, (((0,), (0,)), ((), ())), preferred_element_type=jnp.float32
    )


def to_windows(grid_in):
    row_count, col_count = (grid_in.shape[0], grid_in.shape[1])
    shaped = grid_in.reshape(row_count // SIDE, SIDE, col_count // SIDE, SIDE, -1)
    return shaped.transpose(0, 2, 1, 3, 4).reshape(-1, WINDOW, grid_in.shape[2])


def from_windows(grid_in, row_count, col_count):
    shaped = grid_in.reshape(row_count // SIDE, col_count // SIDE, SIDE, SIDE, -1)
    return shaped.transpose(0, 2, 1, 3, 4).reshape(row_count * col_count, -1)


def to_shifted(grid_in):
    lower_rim = from_behind(grid_in[:SHIFT], "ha", -1)
    taller = jnp.concatenate([grid_in[SHIFT:], lower_rim], 0)
    right_rim = from_behind(taller[:, :SHIFT], "wa", -1)
    return jnp.concatenate([taller[:, SHIFT:], right_rim], 1)


def from_shifted(grid_in):
    upper_rim = from_behind(grid_in[-SHIFT:], "ha", 1)
    taller = jnp.concatenate([upper_rim, grid_in[:-SHIFT]], 0)
    left_rim = from_behind(taller[:, -SHIFT:], "wa", 1)
    return jnp.concatenate([left_rim, taller[:, :-SHIFT]], 1)


def attend(qkv_win, region_win, pos_bias):
    win_count = qkv_win.shape[0]
    parts_qkv = qkv_win.reshape(win_count, WINDOW, 3, HEADS, HEAD_DIM)
    queries, keys_in, values = (parts_qkv[:, :, 0], parts_qkv[:, :, 1], parts_qkv[:, :, 2])
    scores = (
        jnp.einsum("wihd,wjhd->whij", queries, keys_in, preferred_element_type=jnp.float32)
        * HEAD_DIM ** (-0.5)
        + pos_bias[None]
    )
    same_region = region_win[:, :, None] == region_win[:, None, :]
    scores = jnp.where(same_region[:, None], scores, -1e30)
    exponent = jnp.exp(scores - jnp.max(scores, -1, keepdims=True))
    attn_probs = exponent / jnp.sum(exponent, -1, keepdims=True)
    probs_low = attn_probs.astype(jnp.bfloat16)
    weighted = jnp.einsum("whij,wjhd->wihd", probs_low, values, preferred_element_type=jnp.float32)
    return (
        weighted.reshape(win_count, WINDOW, HEADS * HEAD_DIM).astype(jnp.bfloat16),
        attn_probs,
        probs_low,
    )


def attend_back(qkv_win, attn_probs, probs_low, upstream):
    win_count = qkv_win.shape[0]
    parts_qkv = qkv_win.reshape(win_count, WINDOW, 3, HEADS, HEAD_DIM)
    queries, keys_in, values = (parts_qkv[:, :, 0], parts_qkv[:, :, 1], parts_qkv[:, :, 2])
    grad_out = upstream.reshape(win_count, WINDOW, HEADS, HEAD_DIM)
    grad_probs = jnp.einsum("wihd,wjhd->whij", grad_out, values, preferred_element_type=jnp.float32)
    grad_values = jnp.einsum(
        "whij,wihd->wjhd", probs_low, grad_out, preferred_element_type=jnp.float32
    )
    grad_scores = attn_probs * (grad_probs - jnp.sum(attn_probs * grad_probs, -1, keepdims=True))
    bias_grad = jnp.sum(grad_scores, 0)
    scaled = (grad_scores * HEAD_DIM ** (-0.5)).astype(jnp.bfloat16)
    grad_queries = jnp.einsum(
        "whij,wjhd->wihd", scaled, keys_in, preferred_element_type=jnp.float32
    )
    grad_keys = jnp.einsum("whij,wihd->wjhd", scaled, queries, preferred_element_type=jnp.float32)
    stacked = jnp.stack([grad_queries, grad_keys, grad_values], 2)
    return (
        stacked.reshape(win_count, WINDOW, 3 * HEADS * HEAD_DIM).astype(jnp.bfloat16),
        bias_grad,
    )


def clip_factor(norm_sq):
    return jnp.minimum(1.0, math.sqrt(PARAMS) / (jnp.sqrt(norm_sq) + 1e-06))


def squares_of(gradients):
    return jnp.sum(jnp.stack([jnp.sum(gradient * gradient) for gradient in gradients]))


def local(tokens, cotangent, w_qkv, w_proj, w_fc1, w_fc2, bias_table, rel_index, region):
    tile_rows, tile_cols, channels = tokens.shape
    lookup = (rel_index.reshape(-1)[:, None] == jnp.arange(TABLE, dtype=jnp.int32)[None, :]).astype(
        jnp.float32
    )
    pos_bias = jnp.dot(lookup, bias_table, precision=highest).T.reshape(HEADS, WINDOW, WINDOW)
    token_f32 = tokens.astype(jnp.float32)
    first_norm, first_scale = normalize(token_f32)
    shifted = to_shifted(first_norm.astype(jnp.bfloat16))
    flat_shift = shifted.reshape(-1, channels)
    qkv_tok = jnp.dot(flat_shift, w_qkv, preferred_element_type=jnp.float32).astype(jnp.bfloat16)
    qkv_win = to_windows(qkv_tok.reshape(tile_rows, tile_cols, 3 * channels))
    region_win = to_windows(region[..., None])[..., 0]
    attn_win, attn_probs, probs_low = attend(qkv_win, region_win, pos_bias)
    attn_tok = from_windows(attn_win, tile_rows, tile_cols)
    projected = jnp.dot(attn_tok, w_proj, preferred_element_type=jnp.float32).astype(jnp.bfloat16)
    middle = token_f32 + from_shifted(projected.reshape(tile_rows, tile_cols, channels)).astype(
        jnp.float32
    )
    second_norm, second_scale = normalize(middle)
    normed_low = second_norm.astype(jnp.bfloat16).reshape(-1, channels)
    pre_act = jnp.dot(normed_low, w_fc1, preferred_element_type=jnp.float32)
    activated = jax.nn.gelu(pre_act, approximate=False).astype(jnp.bfloat16)
    block_out = (
        middle
        + jnp.dot(activated, w_fc2, preferred_element_type=jnp.float32).reshape(
            tile_rows, tile_cols, channels
        )
    ).astype(jnp.bfloat16)
    upstream = cotangent.reshape(-1, channels)
    grad_fc2 = contract(activated, upstream)
    grad_pre = (
        jnp.dot(upstream, w_fc2.T, preferred_element_type=jnp.float32) * gelu_slope(pre_act)
    ).astype(jnp.bfloat16)
    grad_fc1 = contract(normed_low, grad_pre)
    grad_second = jnp.dot(grad_pre, w_fc1.T, preferred_element_type=jnp.float32).reshape(
        tile_rows, tile_cols, channels
    )
    grad_mid = cotangent.astype(jnp.float32) + normalize_back(
        second_norm, second_scale, grad_second
    )
    back_rolled = to_shifted(grad_mid.astype(jnp.bfloat16)).reshape(-1, channels)
    grad_proj = contract(attn_tok, back_rolled)
    grad_attn = jnp.dot(back_rolled, w_proj.T, preferred_element_type=jnp.float32).astype(
        jnp.bfloat16
    )
    attn_back = to_windows(grad_attn.reshape(tile_rows, tile_cols, channels))
    qkv_grads, bias_grad = attend_back(qkv_win, attn_probs, probs_low, attn_back)
    grad_table = jnp.dot(lookup.T, bias_grad.reshape(HEADS, -1).T, precision=highest)
    qkv_back = from_windows(qkv_grads, tile_rows, tile_cols)
    grad_qkv = contract(flat_shift, qkv_back)
    grad_shift = jnp.dot(qkv_back, w_qkv.T, preferred_element_type=jnp.float32).astype(jnp.bfloat16)
    grad_normed = from_shifted(grad_shift.reshape(tile_rows, tile_cols, channels))
    token_grad = (
        grad_mid + normalize_back(first_norm, first_scale, grad_normed.astype(jnp.float32))
    ).astype(jnp.bfloat16)
    summed = lax.psum((grad_qkv, grad_proj, grad_fc1, grad_fc2, grad_table), ("ha", "wa"))
    factor = clip_factor(squares_of(summed))
    clipped = tuple((gradient * factor for gradient in summed))
    return (block_out, token_grad, clipped[0], clipped[1], clipped[2], clipped[3], clipped[4])


def solution(mesh):
    placed = (P("ha", "wa", None), P("ha", "wa", None), P(), P(), P(), P(), P(), P(), P("ha", "wa"))
    return jax.shard_map(
        local,
        mesh=mesh,
        in_specs=placed,
        out_specs=(P("ha", "wa", None), P("ha", "wa", None), P(), P(), P(), P(), P()),
        check_vma=False,
    )
```

profile of v0, /device:TPU:0, one launch (start us, length us, event | category | flops | bytes accessed | tf_op | source)
XLA Modules:
  0.0 435.5 jit_solution(15987146549414626448)
XLA Ops:
  11.6 4.0 collective-permute-start
  18.6 2.8 collective-permute-start.1
  23.8 3.8 convolution_convert_fusion
  27.6 4.0 reshape_reshape.13
  31.6 3.5 copy.56
  35.1 11.7 %reshape_reshape.14 = bf16[16,49,3,12,32]{4,3,2,0,1:T(8,128)(2,1)} reshape(bf16[4,4,7,7,1152]{4,1,0,3,2:T(4,128)(2,1)} %copy.56) | data formatting | bytes 3612672 | tf_op jit(solution)/shard_map/reshape;reshape | solution.py:77
  46.9 8.5 %fusion.76 = (bf16[16,49,1,12,32]{4,3,2,0,1:T(8,128)(2,1)}, bf16[16,49,1,12,32]{4,3,2,0,1:T(8,128)(2,1)}, bf16[16,49,1,12,32]{4,3,2,0,1:T(8,128)(2,1)}) fusion(bf16[16,49,3,12,32]{4,3,2,0,1:T(8,128)(2,1)} %reshape_reshape.14), kind=kLoop, calls=%fused_computation.130 | loop fusion | bytes 3612672 | tf_op jit(solution)/shard_map/slice | solution.py:78
  55.3 5.4 %copy.79 = bf16[16,49,1,12,32]{1,4,3,0,2:T(8,128)(2,1)} copy(bf16[16,49,1,12,32]{4,3,2,0,1:T(8,128)(2,1)} %get-tuple-element.13) | data formatting | bytes 1204224
  60.7 5.4 %copy.80 = bf16[16,49,1,12,32]{1,4,3,0,2:T(8,128)(2,1)} copy(bf16[16,49,1,12,32]{4,3,2,0,1:T(8,128)(2,1)} %get-tuple-element.15) | data formatting | bytes 1204224
  66.1 5.4 %copy.78 = bf16[16,49,1,12,32]{1,4,3,0,2:T(8,128)(2,1)} copy(bf16[16,49,1,12,32]{4,3,2,0,1:T(8,128)(2,1)} %get-tuple-element.14) | data formatting | bytes 1204224
  71.5 3.6 fusion.32
  77.2 2.4 copy-done.31
  79.7 2.2 fusion.39
  81.8 7.1 %copy.63 = bf16[16,49,12,32]{3,2,0,1:T(8,128)(2,1)} copy(bf16[16,49,12,32]{1,3,2,0:T(8,128)(2,1)} %fusion.39) | data formatting | bytes 1204224 | tf_op jit(solution)/shard_map/convert_element_type | solution.py:91
  89.0 4.7 %convert_element_type.73 = bf16[4,4,7,7,384]{4,1,0,3,2:T(4,128)(2,1)S(1)} reshape(bf16[16,49,12,32]{3,2,0,1:T(8,128)(2,1)} %copy.63) | data formatting | bytes 1204224 | tf_op jit(solution)/shard_map/convert_element_type | solution.py:91
  104.1 4.7 %collective-permute-done.3 = bf16[28,3,384]{2,1,0:T(4,128)(2,1)S(1)} collective-permute-done((bf16[28,3,384]{2,1,0:T(4,128)(2,1)S(1)}, bf16[28,3,384]{2,1,0:T(4,128)(2,1)S(1)}, u32[]{:S(2)}, u32[]{:S(2)}) %collective-permute-start.3) | collective-permute-done | bytes 64544 | tf_op jit(solution)/shard_map/ppermute | solution.py:23
  113.4 13.0 %fusion.5 = (bf16[784,1536]{1,0:T(8,128)(2,1)}, f32[784,1536]{1,0:T(8,128)S(1)}) fusion(bf16[784,384]{1,0:T(8,128)(2,1)} %reshape.116, bf16[384,1536]{1,0:T(8,128)(2,1)S(1)} %copy-done), kind=kOutput, calls=%fused_computation.12 | convolution fusion | flops 1003118592 | bytes 9007104 | tf_op jit(solution)/shard_map/dot_general | solution.py:149
  126.5 2.7 fusion.11
  129.2 2.5 fusion.78
  131.7 2.8 fusion.83
  134.5 2.4 reshape.119
  139.1 2.3 fusion.69
  142.1 3.2 fusion.84
  149.3 2.5 convolution_convert_fusion.6
  151.7 2.6 fusion.82
  156.8 4.9 %reshape_reshape.16 = bf16[16,49,12,32]{3,2,0,1:T(8,128)(2,1)} reshape(bf16[4,4,7,7,384]{4,1,0,3,2:T(4,128)(2,1)} %copy.65) | data formatting | bytes 1204224 | tf_op jit(solution)/shard_map/reshape;reshape | solution.py:101
  161.6 5.4 %copy.66 = bf16[16,49,12,32]{1,3,2,0:T(8,128)(2,1)} copy(bf16[16,49,12,32]{3,2,0,1:T(8,128)(2,1)} %reshape_reshape.16) | data formatting | bytes 1204224 | tf_op jit(solution)/shard_map/reshape;reshape | solution.py:101
  167.0 5.9 %fusion.36 = f32[16,12,49,49]{2,3,1,0:T(8,128)} fusion(bf16[16,49,12,32]{1,3,2,0:T(8,128)(2,1)} %copy.66, bf16[16,49,1,12,32]{1,4,3,0,2:T(8,128)(2,1)} %copy.78), kind=kOutput, calls=%fused_computation.67 | convolution fusion | flops 29503488 | bytes 3048192 | tf_op jit(solution)/shard_map/wihd,wjhd->whij/dot_general | solution.py:102
  172.9 11.0 %fusion.42 = bf16[16,49,1,12,32]{1,4,3,0,2:T(8,128)(2,1)} fusion(bf16[16,49,1,12,32]{1,4,3,0,2:T(8,128)(2,1)} %copy.80, f32[16,12,49,49]{2,3,1,0:T(8,128)} %fusion.36, f32[16,12,49,49]{2,3,1,0:T(8,128)} %copy-done.31, f32[16,12,49]{2,1,0:T(8,128)S(1)} %copy-done.33), kind=kOutput, calls=%fused_computation.71 | convolution fusion | flops 33040944 | bytes 4929792 | tf_op jit(solution)/shard_map/whij,wjhd->wihd/dot_general | solution.py:109
  184.0 10.8 %fusion.45 = bf16[16,49,1,12,32]{1,4,3,0,2:T(8,128)(2,1)} fusion(bf16[16,49,1,12,32]{1,4,3,0,2:T(8,128)(2,1)} %copy.79, f32[16,12,49,49]{2,3,1,0:T(8,128)} %fusion.36, f32[16,12,49,49]{2,3,1,0:T(8,128)} %copy-done.31, f32[16,12,49]{2,1,0:T(8,128)S(1)} %copy-done.33), kind=kOutput, calls=%fused_computation.72 | convolution fusion | flops 33040944 | bytes 4929792 | tf_op jit(solution)/shard_map/whij,wihd->wjhd/dot_general | solution.py:112
  194.8 4.7 %fusion.48 = bf16[16,49,1,12,32]{1,4,3,0,2:T(8,128)(2,1)S(1)} fusion(bf16[16,49,12,32]{1,3,2,0:T(8,128)(2,1)} %copy.66, f32[16,12,49,49]{2,3,1,0:T(8,128)} %copy-done.31, f32[16,12,49]{2,1,0:T(8,128)S(1)} %copy-done.33), kind=kOutput, calls=%fused_computation.73 | convolution fusion | flops 30726528 | bytes 3085824 | tf_op jit(solution)/shard_map/whij,wihd->wjhd/dot_general | solution.py:103
  199.6 2.7 pad_maximum_fusion
  202.3 17.7 %copy.71 = bf16[16,49,3,12,32]{4,3,2,0,1:T(8,128)(2,1)} copy(bf16[16,49,3,12,32]{1,4,3,0,2:T(8,128)(2,1)} %pad_maximum_fusion) | data formatting | bytes 3612672 | tf_op jit(solution)/shard_map/stack | solution.py:113
  220.0 12.5 %convert_element_type.84 = bf16[4,4,7,7,1152]{4,1,0,3,2:T(4,128)(2,1)} reshape(bf16[16,49,3,12,32]{4,3,2,0,1:T(8,128)(2,1)} %copy.71) | data formatting | bytes 3612672 | tf_op jit(solution)/shard_map/convert_element_type | solution.py:115
  232.6 3.2 copy.72
  235.8 3.9 reshape.121
  239.7 3.9 fusion.81
  244.8 4.1 fusion.80
  248.9 2.8 reshape.117
  251.7 9.5 %fusion.79 = f32[12,49,49]{1,2,0:T(8,128)S(1)} fusion(f32[16,12,49,49]{2,3,1,0:T(8,128)} %fusion.36, f32[16,12,49,49]{2,3,1,0:T(8,128)} %copy-done.31, f32[16,12,49]{2,1,0:T(8,128)S(1)} %copy-done.33), kind=kOutput, calls=%fused_computation.133 | output fusion | flops 2746596 | bytes 3840816 | tf_op jit(solution)/shard_map/sub | solution.py:106
  261.6 3.0 convolution_convert_fusion.5
  267.2 39.0 %psum.39 = f32[169,12]{0,1:T(8,128)S(1)} all-reduce(f32[169,12]{0,1:T(8,128)S(1)} %fusion.26), channel_id=1, replica_groups=mesh['ha'=4,'wa'=8] {'ha','wa'}, use_global_device_ids=true, to_apply=%region_20.21 | all-reduce | flops 2028 | bytes 16224 | tf_op jit(solution)/shard_map/psum | solution.py:184
  309.0 5.1 %collective-permute-done.7 = bf16[28,3,384]{2,1,0:T(4,128)(2,1)S(1)} collective-permute-done((bf16[28,3,384]{2,1,0:T(4,128)(2,1)S(1)}, bf16[28,3,384]{2,1,0:T(4,128)(2,1)S(1)}, u32[]{:S(2)}, u32[]{:S(2)}) %collective-permute-start.7) | collective-permute-done | bytes 64544 | tf_op jit(solution)/shard_map/ppermute | solution.py:23
  315.2 4.2 fusion.52
  319.4 89.5 %all-reduce.3.cloned.1.call-done = (f32[384,1152]{1,0:T(8,128)}, f32[384,384]{1,0:T(8,128)}, f32[384,1536]{1,0:T(8,128)}, f32[1536,384]{1,0:T(8,128)}) async-done(((f32[384,1152]{1,0:T(8,128)}, f32[384,384]{1,0:T(8,128)}, f32[384,1536]{1,0:T(8,128)}, f32[1536,384]{1,0:T(8,128)}), (f32[384,1152]{1,0:T(8,128)}, f32[384,384]{1,0:T(8,128)}, f32[384,1536]{1,0:T(8,128)}, ...) | async-done | bytes 7077904 | tf_op jit(solution)/shard_map/psum | solution.py:184
  408.8 2.7 multiply_reduce_fusion.3
  419.6 3.2 broadcast_multiply_fusion
  422.8 3.4 broadcast_multiply_fusion.1
  (149 shorter events, 51.0 us)
Async XLA Ops:
  7.2 106.2 %copy-start = (bf16[384,1536]{1,0:T(8,128)(2,1)S(1)}, bf16[384,1536]{1,0:T(8,128)(2,1)}, u32[]{:S(2)}) copy-start(bf16[384,1536]{1,0:T(8,128)(2,1)} %param.13) | copy-start | bytes 3538948
  7.2 8.4 %copy-start.23 = (s32[49,49]{1,0:T(8,128)S(1)}, s32[49,49]{1,0:T(8,128)}, u32[]{:S(2)}) copy-start(s32[49,49]{1,0:T(8,128)} %param.16) | copy-start | bytes 28816
  7.2 8.5 %copy-start.24 = (s32[28,28]{1,0:T(8,128)S(1)}, s32[28,28]{1,0:T(8,128)}, u32[]{:S(2)}) copy-start(s32[28,28]{1,0:T(8,128)} %param.17) | copy-start | bytes 9412
  7.2 8.7 %copy-start.29 = (f32[169,12]{0,1:T(8,128)S(1)}, f32[169,12]{0,1:T(8,128)}, u32[]{:S(2)}) copy-start(f32[169,12]{0,1:T(8,128)} %param.15) | copy-start | bytes 24340
  7.2 401.6 %all-reduce.3.cloned.1.call-start = ((), (), s32[]{:S(2)}) async-start(), calls=%async_computation | async-start | bytes 14155776 | tf_op jit(solution)/shard_map/psum | solution.py:184
  8.7 9.0 %copy-start.18 = (f32[28,28]{1,0:T(8,128)}, f32[28,28]{1,0:T(8,128)S(1)}, u32[]{:S(2)}) copy-start(f32[28,28]{1,0:T(8,128)S(1)} %broadcast_multiply_fusion.9) | copy-start | bytes 9412
  10.2 8.4 %copy-start.21 = (f32[28,28]{1,0:T(8,128)}, f32[28,28]{1,0:T(8,128)S(1)}, u32[]{:S(2)}) copy-start(f32[28,28]{1,0:T(8,128)S(1)} %add_rsqrt_fusion.1) | copy-start | bytes 9412
  11.6 7.0 %collective-permute-start = (bf16[3,28,384]{2,1,0:T(8,128)(2,1)S(1)}, bf16[3,28,384]{2,1,0:T(8,128)(2,1)S(1)}, u32[]{:S(2)}, u32[]{:S(2)}) collective-permute-start(bf16[3,28,384]{2,1,0:T(8,128)(2,1)S(1)} %slice.96), channel_id=1, source_target_pairs={{0,24},{8,0},{16,8},{24,16},{1,25},{9,1},{17,9},{25,17},{2,26},{10... | collective-permute-start | bytes 193544 | tf_op jit(solution)/shard_map/ppermute | solution.py:23
  15.7 1.5 copy-start.25
  18.6 4.9 %collective-permute-start.1 = (bf16[28,3,384]{2,1,0:T(4,128)(2,1)S(1)}, bf16[28,3,384]{2,1,0:T(4,128)(2,1)S(1)}, u32[]{:S(2)}, u32[]{:S(2)}) collective-permute-start(bf16[28,3,384]{2,1,0:T(4,128)(2,1)S(1)} %pad_maximum_fusion.6), channel_id=1, source_target_pairs={{0,7},{1,0},{2,1},{3,2},{4,3},{5,4},{6,5},{7,6},{8,15},{9,8},{10,9... | collective-permute-start | bytes 193544 | tf_op jit(solution)/shard_map/ppermute | solution.py:23
  23.8 3.8 copy-start.14
  71.5 3.6 copy-start.20
  75.1 4.6 %copy-start.6 = (bf16[16,49,1,12,32]{1,4,3,0,2:T(8,128)(2,1)S(1)}, bf16[16,49,1,12,32]{1,4,3,0,2:T(8,128)(2,1)}, u32[]{:S(2)}) copy-start(bf16[16,49,1,12,32]{1,4,3,0,2:T(8,128)(2,1)} %copy.78) | copy-start | bytes 1806340
  77.2 2.5 copy-start.31
  77.2 4.6 %copy-start.32 = (f32[16,12,49]{2,1,0:T(8,128)}, f32[16,12,49]{2,1,0:T(8,128)S(1)}, u32[]{:S(2)}) copy-start(f32[16,12,49]{2,1,0:T(8,128)S(1)} %get-tuple-element.18) | copy-start | bytes 112900
  88.9 5.8 %copy-start.12 = (bf16[384,384]{1,0:T(8,128)(2,1)S(1)}, bf16[384,384]{1,0:T(8,128)(2,1)}, u32[]{:S(2)}) copy-start(bf16[384,384]{1,0:T(8,128)(2,1)} %param.12) | copy-start | bytes 884740
  94.8 8.4 %copy-start.7 = (bf16[28,28,384]{2,1,0:T(8,128)(2,1)S(1)}, bf16[28,28,384]{2,1,0:T(8,128)(2,1)}, u32[]{:S(2)}) copy-start(bf16[28,28,384]{2,1,0:T(8,128)(2,1)} %param.10) | copy-start | bytes 1806340
  96.5 12.3 %copy-start.2 = (bf16[28,28,384]{2,1,0:T(8,128)(2,1)S(1)}, bf16[28,28,384]{2,1,0:T(8,128)(2,1)}, u32[]{:S(2)}) copy-start(bf16[28,28,384]{2,1,0:T(8,128)(2,1)} %param.9) | copy-start | bytes 1806340
  96.6 5.3 %collective-permute-start.2 = (bf16[3,28,384]{2,1,0:T(8,128)(2,1)S(1)}, bf16[3,28,384]{2,1,0:T(8,128)(2,1)S(1)}, u32[]{:S(2)}, u32[]{:S(2)}) collective-permute-start(bf16[3,28,384]{2,1,0:T(8,128)(2,1)S(1)} %slice.80), channel_id=1, source_target_pairs={{0,8},{8,16},{16,24},{24,0},{1,9},{9,17},{17,25},{25,1},{2,10},{10... | collective-permute-start | bytes 193544 | tf_op jit(solution)/shard_map/ppermute | solution.py:23
  103.1 5.8 %collective-permute-start.3 = (bf16[28,3,384]{2,1,0:T(4,128)(2,1)S(1)}, bf16[28,3,384]{2,1,0:T(4,128)(2,1)S(1)}, u32[]{:S(2)}, u32[]{:S(2)}) collective-permute-start(bf16[28,3,384]{2,1,0:T(4,128)(2,1)S(1)} %slice.104), channel_id=1, source_target_pairs={{0,1},{1,2},{2,3},{3,4},{4,5},{5,6},{6,7},{7,0},{8,9},{9,10},{10,1... | collective-permute-start | bytes 193544 | tf_op jit(solution)/shard_map/ppermute | solution.py:23
  113.4 13.0 %copy-start.16 = (bf16[784,384]{1,0:T(8,128)(2,1)S(1)}, bf16[784,384]{1,0:T(8,128)(2,1)}, u32[]{:S(2)}) copy-start(bf16[784,384]{1,0:T(8,128)(2,1)} %reshape.118) | copy-start | bytes 1806340
  113.4 13.0 %copy-start.27 = (bf16[1536,384]{1,0:T(8,128)(2,1)S(1)}, bf16[1536,384]{1,0:T(8,128)(2,1)}, u32[]{:S(2)}) copy-start(bf16[1536,384]{1,0:T(8,128)(2,1)} %param.14) | copy-start | bytes 3538948
  129.2 2.5 copy-start.8
  139.0 3.2 copy-start.17
  139.1 3.0 copy-start.30
  141.4 4.6 %collective-permute-start.4 = (bf16[3,28,384]{2,1,0:T(8,128)(2,1)S(1)}, bf16[3,28,384]{2,1,0:T(8,128)(2,1)S(1)}, u32[]{:S(2)}, u32[]{:S(2)}) collective-permute-start(bf16[3,28,384]{2,1,0:T(8,128)(2,1)S(1)} %slice.107), channel_id=1, source_target_pairs={{0,24},{8,0},{16,8},{24,16},{1,25},{9,1},{17,9},{25,17},{2,26},{10... | collective-permute-start | bytes 193544 | tf_op jit(solution)/shard_map/ppermute | solution.py:23
  145.4 3.9 copy-start.13
  146.0 2.2 collective-permute-start.5
  167.0 5.9 %copy-start.33 = (f32[16,12,49]{2,1,0:T(8,128)S(1)}, f32[16,12,49]{2,1,0:T(8,128)}, u32[]{:S(2)}) copy-start(f32[16,12,49]{2,1,0:T(8,128)} %copy-done.32) | copy-start | bytes 112900
  194.8 4.7 %copy-start.10 = (bf16[16,49,1,12,32]{1,4,3,0,2:T(8,128)(2,1)S(1)}, bf16[16,49,1,12,32]{1,4,3,0,2:T(8,128)(2,1)}, u32[]{:S(2)}) copy-start(bf16[16,49,1,12,32]{1,4,3,0,2:T(8,128)(2,1)} %fusion.42) | copy-start | bytes 1806340
  194.8 4.7 %copy-start.11 = (bf16[16,49,1,12,32]{1,4,3,0,2:T(8,128)(2,1)S(1)}, bf16[16,49,1,12,32]{1,4,3,0,2:T(8,128)(2,1)}, u32[]{:S(2)}) copy-start(bf16[16,49,1,12,32]{1,4,3,0,2:T(8,128)(2,1)} %fusion.45) | copy-start | bytes 1806340
  235.8 3.9 copy-start.15
  243.6 1.3 copy-start.28
  261.6 3.7 copy-start.26
  264.6 49.6 %copy-start.19 = (f32[28,28]{1,0:T(8,128)S(1)}, f32[28,28]{1,0:T(8,128)}, u32[]{:S(2)}) copy-start(f32[28,28]{1,0:T(8,128)} %copy-done.18) | copy-start | bytes 9412
  264.6 49.5 %copy-start.22 = (f32[28,28]{1,0:T(8,128)S(1)}, f32[28,28]{1,0:T(8,128)}, u32[]{:S(2)}) copy-start(f32[28,28]{1,0:T(8,128)} %copy-done.21) | copy-start | bytes 9412
  264.6 41.6 %collective-permute-start.6 = (bf16[3,28,384]{2,1,0:T(8,128)(2,1)S(1)}, bf16[3,28,384]{2,1,0:T(8,128)(2,1)}, u32[]{:S(2)}, u32[]{:S(2)}) collective-permute-start(bf16[3,28,384]{2,1,0:T(8,128)(2,1)S(1)} %slice.90), channel_id=1, source_target_pairs={{0,8},{8,16},{16,24},{24,0},{1,9},{9,17},{17,25},{25,1},{2,10},{10... | collective-permute-start | bytes 193544 | tf_op jit(solution)/shard_map/ppermute | solution.py:23
  308.4 5.8 %collective-permute-start.7 = (bf16[28,3,384]{2,1,0:T(4,128)(2,1)S(1)}, bf16[28,3,384]{2,1,0:T(4,128)(2,1)S(1)}, u32[]{:S(2)}, u32[]{:S(2)}) collective-permute-start(bf16[28,3,384]{2,1,0:T(4,128)(2,1)S(1)} %slice.112), channel_id=1, source_target_pairs={{0,1},{1,2},{2,3},{3,4},{4,5},{5,6},{6,7},{7,0},{8,9},{9,10},{10,1... | collective-permute-start | bytes 193544 | tf_op jit(solution)/shard_map/ppermute | solution.py:23
  408.8 4.5 %copy-start.3 = (f32[384,1536]{1,0:T(8,128)S(1)}, f32[384,1536]{1,0:T(8,128)}, u32[]{:S(2)}) copy-start(f32[384,1536]{1,0:T(8,128)} %get-tuple-element.11) | copy-start | bytes 7077892
  408.8 5.7 %copy-start.4 = (f32[1536,384]{1,0:T(8,128)S(1)}, f32[1536,384]{1,0:T(8,128)}, u32[]{:S(2)}) copy-start(f32[1536,384]{1,0:T(8,128)} %get-tuple-element.12) | copy-start | bytes 7077892
  422.8 3.4 copy-start.9
  422.8 4.2 copy-start.5
  422.8 5.6 %copy-start.1 = (bf16[384,1536]{1,0:T(8,128)(2,1)S(1)}, bf16[384,1536]{1,0:T(8,128)(2,1)}, u32[]{:S(2)}) copy-start(bf16[384,1536]{1,0:T(8,128)(2,1)} %param.13) | copy-start | bytes 3538948
Sparse Core Ops, SparseCore 0:
  243.7 165.0 all-reduce.2
where the time goes:
time: 441 us; the launch traced here: 436 us
  local copies, waits for them, and re-layouts  129 us (29%)
  waiting for transfers between devices  106 us (24%)
  matrix products  86.2 us (20%)
  other arithmetic  48.5 us (11%)
  blocking collectives  39 us (9%)
  between operations  18.2 us (4%)
  starting transfers between devices  8.84 us (2%)
    psum x1, waiting for transfers between devices, local(): lax.psum((grad_qkv, grad_proj, grad_fc1, grad_fc2, grad_table), ('ha', 'w...  89.5 us
    psum x1, blocking collectives, local(): lax.psum((grad_qkv, grad_proj, grad_fc1, grad_fc2, grad_table), ('ha', 'w...  39 us
    unnamed x73, local copies, waits for them, and re-layouts  20.9 us
    another operation x1, local copies, waits for them, and re-layouts, attend_back(): stacked = jnp.stack([grad_queries, grad_keys, grad_values], 2)  17.7 us
    ppermute x8, waiting for transfers between devices, from_behind(): return lax.ppermute(x, axis, [(i, (i + by) % count) for i in range(count)])  16.2 us
    dot_general x1, matrix products, local(): pre_act = jnp.dot(normed_low, w_fc1, preferred_element_type=jnp.float32)  13 us
    convert_element_type x1, local copies, waits for them, and re-layouts, attend_back(): stacked.reshape(win_count, WINDOW, 3 * HEADS * HEAD_DIM)  12.5 us
    dot_general x4, matrix products, contract(): lax.dot_general(left_in, right_in, (((0,), (0,)), ((), ())), preferred_el...  12.5 us
  transfers between devices with their start and end apart: 9, of which 7 were waited for; matrix products, arithmetic and copies ran while one was open for 9% of the time, Pallas kernels for 0%

commit v1 on v0

v1 whole, which is shorter than its diff:
```python
import functools
import math

import jax
import jax.numpy as jnp
from jax import lax
from jax.experimental import pallas as pl
from jax.experimental.pallas import tpu as pltpu
from jax.sharding import PartitionSpec as P

HEADS = 12
SIDE = 7
SHIFT = 3
HEAD_DIM = 32
TABLE = 169
PARAMS = 1771500
CELL = 8
SLOTS = CELL * CELL
GROUP = 4
LANES = GROUP * HEAD_DIM
GROUPS = HEADS // GROUP
FFN_CHUNKS = 3

epsilon = 1e-05
highest = lax.Precision.HIGHEST
f32 = jnp.float32
bf16 = jnp.bfloat16


def from_behind(x, axis, by):
    count = lax.axis_size(axis)
    return lax.ppermute(x, axis, [(i, (i + by) % count) for i in range(count)])


def to_shifted(grid_in):
    lower_rim = from_behind(grid_in[:SHIFT], "ha", -1)
    taller = jnp.concatenate([grid_in[SHIFT:], lower_rim], 0)
    right_rim = from_behind(taller[:, :SHIFT], "wa", -1)
    return jnp.concatenate([taller[:, SHIFT:], right_rim], 1)


def from_shifted(grid_in):
    upper_rim = from_behind(grid_in[-SHIFT:], "ha", 1)
    taller = jnp.concatenate([upper_rim, grid_in[:-SHIFT]], 0)
    left_rim = from_behind(taller[:, -SHIFT:], "wa", 1)
    return jnp.concatenate([left_rim, taller[:, :-SHIFT]], 1)


def to_cells(grid_in, fill):
    rows, cols, channels = grid_in.shape
    split = grid_in.reshape(rows // SIDE, SIDE, cols // SIDE, SIDE, channels)
    extra = CELL - SIDE
    padded = jnp.pad(
        split, ((0, 0), (0, extra), (0, 0), (0, extra), (0, 0)), constant_values=fill
    )
    return padded.transpose(0, 2, 1, 3, 4).reshape(-1, channels)


def from_cells(flat, rows, cols):
    split = flat.reshape(rows // SIDE, cols // SIDE, CELL, CELL, -1)[:, :, :SIDE, :SIDE]
    return split.transpose(0, 2, 1, 3, 4).reshape(rows, cols, -1)


def normalize(values):
    average = jnp.mean(values, -1, keepdims=True)
    centred = values - average
    inverse = lax.rsqrt(jnp.mean(centred * centred, -1, keepdims=True) + epsilon)
    return (centred * inverse, inverse)


def normalize_back(normal_rows, inverse, upstream):
    up_mean = jnp.mean(upstream, -1, keepdims=True)
    cross_mean = jnp.mean(upstream * normal_rows, -1, keepdims=True)
    return inverse * (upstream - up_mean - normal_rows * cross_mean)


def product(left, right, left_dim, right_dim):
    return lax.dot_general(
        left, right, (((left_dim,), (right_dim,)), ((), ())), preferred_element_type=f32
    )


def head_mask():
    shape = (GROUP * SLOTS, LANES)
    row_head = lax.broadcasted_iota(jnp.int32, shape, 0) // SLOTS
    lane_head = lax.broadcasted_iota(jnp.int32, shape, 1) // HEAD_DIM
    return (row_head == lane_head).astype(f32)


def stack_heads(rows, mask):
    return jnp.concatenate([rows] * GROUP, 0) * mask


def gather_heads(stacked, mask):
    kept = stacked * mask
    total = kept[:SLOTS]
    for head in range(1, GROUP):
        total = total + kept[head * SLOTS : (head + 1) * SLOTS]
    return total


def forward_kernel(
    windows, steps, tok_ref, ct_ref, col_ref, row_ref, bias_ref, wq_ref, wp_ref, w1_ref, w2_ref,
    out_ref, mid_ref, qkv_ref, attn_ref, probs_ref, g1_ref, g2_ref, acc1, acc2,
):
    step = pl.program_id(0)

    @pl.when(step == 0)
    def _():
        acc1[...] = jnp.zeros_like(acc1)
        acc2[...] = jnp.zeros_like(acc2)

    channels = tok_ref.shape[1]
    token = tok_ref[...].astype(f32)
    normal, _ = normalize(token)
    qkv_ref[...] = product(normal.astype(bf16), wq_ref[...], 1, 0).astype(bf16)
    mask = head_mask()
    mask_low = mask.astype(bf16)
    for w in range(windows):
        at = slice(w * SLOTS, (w + 1) * SLOTS)
        same = col_ref[at, :] == row_ref[w]
        hidden = jnp.where(same, 0.0, -1e30)
        hidden = jnp.concatenate([hidden] * GROUP, 0)
        for g in range(GROUPS):
            lanes = g * LANES
            query = stack_heads(qkv_ref[at, lanes : lanes + LANES], mask_low)
            key = qkv_ref[at, channels + lanes : channels + lanes + LANES]
            value = qkv_ref[at, 2 * channels + lanes : 2 * channels + lanes + LANES]
            bias = bias_ref[g * GROUP * SLOTS : (g + 1) * GROUP * SLOTS, :]
            scores = product(query, key, 1, 1) * HEAD_DIM ** (-0.5) + bias + hidden
            exponent = jnp.exp(scores - jnp.max(scores, -1, keepdims=True))
            probs = exponent * (1.0 / jnp.sum(exponent, -1, keepdims=True))
            start = (w * GROUPS + g) * GROUP * SLOTS
            probs_ref[start : start + GROUP * SLOTS, :] = probs
            mixed = product(probs.astype(bf16), value, 1, 0)
            attn_ref[at, lanes : lanes + LANES] = gather_heads(mixed, mask).astype(bf16)
    projected = product(attn_ref[...], wp_ref[...], 1, 0).astype(bf16)
    middle = token + projected.astype(f32)
    second, scale = normalize(middle)
    low = second.astype(bf16)
    upstream = ct_ref[...]
    low_turned = low.T
    up_turned = upstream.T
    hidden_units = w1_ref.shape[1]
    width = hidden_units // FFN_CHUNKS
    total = middle
    back = jnp.zeros_like(middle)
    for c in range(FFN_CHUNKS):
        at = slice(c * width, (c + 1) * width)
        w1 = w1_ref[:, at]
        w2 = w2_ref[at, :]
        pre = product(low, w1, 1, 0)
        cdf = 0.5 * (1.0 + lax.erf(pre * 2.0 ** (-0.5)))
        density = jnp.exp(-0.5 * pre * pre) * (2.0 * math.pi) ** (-0.5)
        active = (pre * cdf).astype(bf16)
        total = total + product(active, w2, 1, 0)
        acc2[:, at] += product(up_turned, active, 1, 0)
        grad_pre = (product(upstream, w2, 1, 1) * (cdf + pre * density)).astype(bf16)
        acc1[:, at] += product(low_turned, grad_pre, 1, 0)
        back = back + product(grad_pre, w1, 1, 1)
    out_ref[...] = total.astype(bf16)
    mid_ref[...] = upstream.astype(f32) + normalize_back(second, scale, back)

    @pl.when(step == steps - 1)
    def _():
        g1_ref[...] = acc1[...].astype(bf16)
        g2_ref[...] = acc2[...].T.astype(bf16)


def backward_kernel(
    windows, steps, tok_ref, mid_ref, qkv_ref, attn_ref, probs_ref, wq_ref, wp_ref,
    grad_ref, packed_ref, table_ref, accq, accp, up_ref, gq_ref,
):
    step = pl.program_id(0)

    @pl.when(step == 0)
    def _():
        accq[...] = jnp.zeros_like(accq)
        accp[...] = jnp.zeros_like(accp)
        table_ref[...] = jnp.zeros_like(table_ref)

    channels = tok_ref.shape[1]
    grad_mid = mid_ref[...]
    low = grad_mid.astype(bf16)
    accp[...] += product(attn_ref[...], low, 0, 0)
    up_ref[...] = product(low, wp_ref[...], 1, 1).astype(bf16)
    mask = head_mask()
    mask_low = mask.astype(bf16)
    for w in range(windows):
        at = slice(w * SLOTS, (w + 1) * SLOTS)
        for g in range(GROUPS):
            first = slice(g * LANES, (g + 1) * LANES)
            second = slice(channels + g * LANES, channels + (g + 1) * LANES)
            third = slice(2 * channels + g * LANES, 2 * channels + (g + 1) * LANES)
            rows = slice(g * GROUP * SLOTS, (g + 1) * GROUP * SLOTS)
            query = stack_heads(qkv_ref[at, first], mask_low)
            key = qkv_ref[at, second]
            value = qkv_ref[at, third]
            upstream = stack_heads(up_ref[at, first], mask_low)
            start = (w * GROUPS + g) * GROUP * SLOTS
            probs = probs_ref[start : start + GROUP * SLOTS, :]
            grad_probs = product(upstream, value, 1, 1)
            inner = jnp.sum(probs * grad_probs, -1, keepdims=True)
            grad_scores = probs * (grad_probs - inner)
            table_ref[rows, :] += grad_scores
            scaled = (grad_scores * HEAD_DIM ** (-0.5)).astype(bf16)
            gq_ref[at, first] = gather_heads(product(scaled, key, 1, 0), mask).astype(bf16)
            gq_ref[at, second] = product(scaled, query, 0, 0).astype(bf16)
            gq_ref[at, third] = product(probs.astype(bf16), upstream, 0, 0).astype(bf16)
    normal, scale = normalize(tok_ref[...].astype(f32))
    grads = gq_ref[...]
    accq[...] += product(normal.astype(bf16), grads, 0, 0)
    grad_normed = product(grads, wq_ref[...], 1, 1).astype(bf16).astype(f32)
    grad_ref[...] = (grad_mid + normalize_back(normal, scale, grad_normed)).astype(bf16)

    @pl.when(step == steps - 1)
    def _():
        packed_ref[...] = jnp.zeros_like(packed_ref)
        packed_ref[:channels, : 3 * channels] = accq[...].astype(bf16)
        packed_ref[:channels, 3 * channels :] = accp[...].astype(bf16)


def rows_of(shape, at=0):
    return pl.BlockSpec(shape, lambda i: (i, at))


def whole(shape):
    return pl.BlockSpec(shape, lambda i: (0,) * len(shape))


def local(tokens, cotangent, w_qkv, w_proj, w_fc1, w_fc2, bias_table, rel_index, region):
    tile_rows, tile_cols, channels = tokens.shape
    ffn = w_fc1.shape[1]
    count = (tile_rows // SIDE) * (tile_cols // SIDE)
    windows = math.gcd(count, 4)
    steps = count // windows
    block = windows * SLOTS
    total = count * SLOTS

    both = to_shifted(jnp.concatenate([tokens, cotangent], -1))
    cells = to_cells(both, 0)
    region_cells = to_cells(region[..., None], -1)
    region_rows = region_cells.reshape(count, 1, SLOTS)

    extra = CELL - SIDE
    places = jnp.pad(
        rel_index.reshape(SIDE, SIDE, SIDE, SIDE), ((0, extra),) * 4, constant_values=-1
    ).reshape(1, SLOTS * SLOTS)
    lookup = (jnp.arange(TABLE, dtype=jnp.int32)[:, None] == places).astype(f32)
    pos_bias = lax.dot_general(
        bias_table, lookup, (((0,), (0,)), ((), ())), precision=highest
    ).reshape(HEADS * SLOTS, SLOTS)

    params = pltpu.CompilerParams(
        dimension_semantics=("arbitrary",), vmem_limit_bytes=60 * 1024 * 1024
    )
    shape = jax.ShapeDtypeStruct
    block_cells, grad_mid, qkv, attn, probs, grad_fc1, grad_fc2 = pl.pallas_call(
        functools.partial(forward_kernel, windows, steps),
        name="forward",
        grid=(steps,),
        in_specs=[
            rows_of((block, channels)),
            rows_of((block, channels), 1),
            rows_of((block, 1)),
            pl.BlockSpec((windows, 1, SLOTS), lambda i: (i, 0, 0)),
            whole((HEADS * SLOTS, SLOTS)),
            whole((channels, 3 * channels)),
            whole((channels, channels)),
            whole((channels, ffn)),
            whole((ffn, channels)),
        ],
        out_specs=[
            rows_of((block, channels)),
            rows_of((block, channels)),
            rows_of((block, 3 * channels)),
            rows_of((block, channels)),
            rows_of((windows * HEADS * SLOTS, SLOTS)),
            whole((channels, ffn)),
            whole((ffn, channels)),
        ],
        out_shape=[
            shape((total, channels), bf16),
            shape((total, channels), f32),
            shape((total, 3 * channels), bf16),
            shape((total, channels), bf16),
            shape((count * HEADS * SLOTS, SLOTS), f32),
            shape((channels, ffn), bf16),
            shape((ffn, channels), bf16),
        ],
        scratch_shapes=[pltpu.VMEM((channels, ffn), f32), pltpu.VMEM((channels, ffn), f32)],
        compiler_params=params,
        cost_estimate=pl.CostEstimate(
            flops=20_000_000_000, bytes_accessed=20_000_000, transcendentals=4_000_000
        ),
    )(cells, cells, region_cells, region_rows, pos_bias, w_qkv, w_proj, w_fc1, w_fc2)
    summed_ffn = lax.psum((grad_fc1, grad_fc2), ("ha", "wa"))
    block_out = from_shifted(from_cells(block_cells, tile_rows, tile_cols))

    packed_rows = channels + 16
    grad_cells, packed, bias_grad = pl.pallas_call(
        functools.partial(backward_kernel, windows, steps),
        name="backward",
        grid=(steps,),
        in_specs=[
            rows_of((block, channels)),
            rows_of((block, channels)),
            rows_of((block, 3 * channels)),
            rows_of((block, channels)),
            rows_of((windows * HEADS * SLOTS, SLOTS)),
            whole((channels, 3 * channels)),
            whole((channels, channels)),
        ],
        out_specs=[
            rows_of((block, channels)),
            whole((packed_rows, 4 * channels)),
            whole((HEADS * SLOTS, SLOTS)),
        ],
        out_shape=[
            shape((total, channels), bf16),
            shape((packed_rows, 4 * channels), bf16),
            shape((HEADS * SLOTS, SLOTS), f32),
        ],
        scratch_shapes=[
            pltpu.VMEM((channels, 3 * channels), f32),
            pltpu.VMEM((channels, channels), f32),
            pltpu.VMEM((block, channels), bf16),
            pltpu.VMEM((block, 3 * channels), bf16),
        ],
        compiler_params=params,
        cost_estimate=pl.CostEstimate(
            flops=16_000_000_000, bytes_accessed=16_000_000, transcendentals=1_000_000
        ),
    )(cells, grad_mid, qkv, attn, probs, w_qkv, w_proj)
    grad_table = lax.dot_general(
        bias_grad.reshape(HEADS, SLOTS * SLOTS), lookup, (((1,), (1,)), ((), ())), precision=highest
    )
    packed = lax.dynamic_update_slice(packed, grad_table.astype(bf16), (channels, 0))
    packed, summed_ffn = lax.optimization_barrier((packed, summed_ffn))
    summed = lax.psum(packed, ("ha", "wa")).astype(f32)
    token_grad = from_shifted(from_cells(grad_cells, tile_rows, tile_cols))

    fc1 = summed_ffn[0].astype(f32)
    fc2 = summed_ffn[1].astype(f32)
    norm_sq = jnp.sum(fc1 * fc1) + jnp.sum(fc2 * fc2) + jnp.sum(summed * summed)
    factor = jnp.minimum(1.0, math.sqrt(PARAMS) / (jnp.sqrt(norm_sq) + 1e-06))
    return (
        block_out,
        token_grad,
        summed[:channels, : 3 * channels] * factor,
        summed[:channels, 3 * channels :] * factor,
        fc1 * factor,
        fc2 * factor,
        summed[channels : channels + HEADS, :TABLE].T * factor,
    )


def solution(mesh):
    placed = (P("ha", "wa", None), P("ha", "wa", None), P(), P(), P(), P(), P(), P(), P("ha", "wa"))
    return jax.shard_map(
        local,
        mesh=mesh,
        in_specs=placed,
        out_specs=(P("ha", "wa", None), P("ha", "wa", None), P(), P(), P(), P(), P()),
        check_vma=False,
    )
```

time: 441 us -> 340 us (0.77); the launches traced: 436 us -> 340 us
  waiting for transfers between devices: 106 us -> 238 us
  local copies, waits for them, and re-layouts: 129 us -> 9.7 us
  matrix products: 86.2 us -> 2.44 us
  Pallas kernels: 0 us -> 50 us
  blocking collectives: 39 us -> 0 us
  other arithmetic: 48.5 us -> 14.3 us
    psum x1 -> x2, waiting for transfers between devices: 89.5 us -> 235 us  [the longest x1 129 us: local(): summed = lax.psum(packed, ('ha', 'wa')).astype(f32)]
    dot_general x20 -> x2, matrix products: 86.2 us -> 2.44 us  [the longest x1 1.41 us: local(): lax.dot_general(bias_grad.reshape(HEADS, SLOTS * SLOTS), lookup, (((1,),...]
    pallas_call x0 -> x2, Pallas kernels: none -> 50 us  [the longest x1 26.8 us: local(): pl.pallas_call(functools.partial(forward_kernel, windows, steps), name='f...]
    another operation x8 -> x3, local copies, waits for them, and re-layouts: 45.1 us -> 0.79 us  [the longest x1 0.69 us: local(): region_rows = region_cells.reshape(count, 1, SLOTS)]
    psum x1 -> x0, blocking collectives: 39 us -> none  [local(): lax.psum((grad_qkv, grad_proj, grad_fc1, grad_fc2, grad_table), ('ha', 'w...]
    convert_element_type x3 -> x0, local copies, waits for them, and re-layouts: 24.3 us -> none  [the longest x1 12.5 us: attend_back(): stacked.reshape(win_count, WINDOW, 3 * HEADS * HEAD_DIM)]
    unnamed x73 -> x23, local copies, waits for them, and re-layouts: 20.9 us -> 2.16 us
    ppermute x8 -> x6, waiting for transfers between devices: 16.2 us -> 3.45 us  [from_behind(): return lax.ppermute(x, axis, [(i, (i + by) % count) for i in range(count)])]
  transfers between devices with their start and end apart: 9 -> 8, of which waited for: 7 -> 5; matrix products, arithmetic and copies ran while one was open for 9% -> 4% of each run, Pallas kernels for 0% -> 7%
where the time goes in v1:
time: 340 us
  waiting for transfers between devices  238 us (70%)
  Pallas kernels  50 us (15%)
  between operations  16.4 us (5%)
  other arithmetic  14.3 us (4%)
  local copies, waits for them, and re-layouts  9.7 us (3%)
  starting transfers between devices  9.19 us (3%)
    psum x1, waiting for transfers between devices, local(): summed = lax.psum(packed, ('ha', 'wa')).astype(f32)  129 us
    psum x1, waiting for transfers between devices, local(): summed_ffn = lax.psum((grad_fc1, grad_fc2), ('ha', 'wa'))  105 us
    pallas_call x1, Pallas kernels, local(): pl.pallas_call(functools.partial(forward_kernel, windows, steps), name='f...  26.8 us
    pallas_call x1, Pallas kernels, local(): pl.pallas_call(functools.partial(backward_kernel, windows, steps), name='...  23.3 us
    ppermute x6, starting transfers between devices, from_behind(): return lax.ppermute(x, axis, [(i, (i + by) % count) for i in range(count)])  8.94 us
  transfers between devices with their start and end apart: 8, of which 5 were waited for; matrix products, arithmetic and copies ran while one was open for 4% of the time, Pallas kernels for 7%

profile of v1, /device:TPU:0, one launch (start us, length us, event | category | flops | bytes accessed | tf_op | source)
XLA Modules:
  0.0 340.1 jit_solution(3399185535853614967)
XLA Ops:
  7.2 1.3 constant_dynamic-update-slice_fusion.1
  8.5 0.1 constant_dynamic-update-slice_fusion
  8.7 4.0 %collective-permute-start = (bf16[3,28,768]{2,1,0:T(8,128)(2,1)S(1)}, bf16[3,28,768]{2,1,0:T(8,128)(2,1)S(1)}, u32[]{:S(2)}, u32[]{:S(2)}) collective-permute-start(bf16[3,28,768]{2,1,0:T(8,128)(2,1)S(1)} %slice.69), channel_id=1, source_target_pairs={{0,24},{8,0},{16,8},{24,16},{1,25},{9,1},{17,9},{25,17},{2,26},{10... | collective-permute-start | bytes 387080 | tf_op jit(solution)/shard_map/ppermute | solution.py:32
  12.7 0.1 reshape_broadcast_in_dim.3
  12.8 0.7 reshape_reshape.3.row_ref
  13.5 1.0 reshape.56.col_ref
  14.5 0.1 slice.68
  14.6 0.1 reshape.49
  14.7 0.1 eq.16
  14.9 1.0 convolution_bitcast_fusion
  15.9 0.9 reshape.50.bias_ref
  16.9 2.8 collective-permute-start.1
  19.7 0.4 slice_maximum_fusion
  20.1 2.5 collective-permute-done.1
  22.6 0.2 pad_maximum_fusion
  22.8 0.4 reshape.46
  23.3 0.3 pad_bitcast_fusion
  23.6 1.3 copy.20
  24.9 26.8 %forward.1 = (bf16[1024,384]{1,0:T(8,128)(2,1)}, f32[1024,384]{1,0:T(8,128)}, bf16[1024,1152]{1,0:T(8,128)(2,1)}, bf16[1024,384]{1,0:T(8,128)(2,1)}, f32[12288,6...) custom-call(bf16[1024,768]{1,0:T(8,128)(2,1)} %bitcast.27, bf16[1024,768]{1,0:T(8,128)(2,1)} %bitcast.28, ...), custom_call_target="tpu_custom_call" | custom-call | flops 20000000000 | bytes 20000000 | tf_op jit(solution)/shard_map/forward/pallas_call | solution.py:258
  51.7 0.2 all-reduce.7.cloned.1.call-start
  51.9 23.3 %backward.1 = (bf16[1024,384]{1,0:T(8,128)(2,1)}, bf16[400,1536]{1,0:T(8,128)(2,1)}, f32[768,64]{1,0:T(8,128)}) custom-call(bf16[1024,768]{1,0:T(8,128)(2,1)} %bitcast.29, f32[1024,384]{1,0:T(8,128)} %get-tuple-element.21.mid_ref, bf16[1024,1152]{1,0:T(8,128)(2,1)} %get-tuple-element.22.qkv_ref, bf16[1024,384]{1,0:T(8,128)(2,1)} %get-tuple-element.23.attn_ref, ...), custom_call_target="tpu_custom_call" | custom-call | flops 16000000000 | bytes 16000000 | tf_op jit(solution)/shard_map/backward/pallas_call | solution.py:301
  75.2 0.1 copy_bitcast_fusion.1
  75.3 0.2 reshape.52
  75.5 0.1 slice.74
  75.6 0.8 copy-done.7
  76.4 0.1 copy_bitcast_fusion
  76.5 0.2 reshape.54
  76.7 0.1 slice.77
  76.8 0.9 collective-permute-start.2
  77.7 1.2 collective-permute-start.4
  78.8 0.1 reshape.55
  79.0 1.4 fusion.5
  80.4 1.5 dynamic_update_slice.3
  81.9 0.2 collective-permute-done.2
  82.2 0.7 collective-permute-done.4
  83.0 105.4 %all-reduce.9.cloned.1.call-done = (bf16[384,1536]{1,0:T(8,128)(2,1)}, bf16[1536,384]{1,0:T(8,128)(2,1)}) async-done(((bf16[384,1536]{1,0:T(8,128)(2,1)}, bf16[1536,384]{1,0:T(8,128)(2,1)}), (bf16[384,1536]{1,0:T(8,128)(2,1)}, bf16[1536,384]{1,0:T(8,128)(2,1)})) %all-reduce.9.cloned.1.call-update) | async-done | bytes 2359312 | tf_op jit(solution)/shard_map/psum | solution.py:297
  188.4 1.1 fusion.7
  189.6 1.1 fusion.6
  190.7 1.2 fusion.2
  191.9 1.2 fusion.1
  194.4 129.2 %all-reduce.7.cloned.1.call-done = bf16[400,1536]{1,0:T(8,128)(2,1)} async-done(((bf16[400,1536]{1,0:T(8,128)(2,1)}), bf16[400,1536]{1,0:T(8,128)(2,1)}) %all-reduce.7.cloned.1.call-update) | async-done | bytes 1228816 | tf_op jit(solution)/shard_map/psum | solution.py:340
  323.6 2.5 multiply_reduce_fusion
  326.9 1.6 convert_multiply_fusion
  328.4 1.7 convert_multiply_fusion.2
  330.2 0.3 convert_element_type.16
  330.5 0.6 fusion.8
  331.1 0.9 slice_multiply_fusion.1
  331.9 1.3 slice_multiply_fusion
  (38 shorter events, 0.5 us)
Async XLA Ops:
  7.2 7.7 %copy-start = (f32[169,12]{0,1:T(8,128)S(1)}, f32[169,12]{0,1:T(8,128)}, u32[]{:S(2)}) copy-start(f32[169,12]{0,1:T(8,128)} %param.15) | copy-start | bytes 24340
  7.2 1.3 copy-start.5
  7.2 5.5 %copy-start.10 = (s32[28,28]{1,0:T(8,128)S(1)}, s32[28,28]{1,0:T(8,128)}, u32[]{:S(2)}) copy-start(s32[28,28]{1,0:T(8,128)} %param.17) | copy-start | bytes 9412
  7.2 181.2 %all-reduce.9.cloned.1.call-start = ((), (), s32[]{:S(2)}) async-start(), calls=%async_computation.1 | async-start | bytes 4718592 | tf_op jit(solution)/shard_map/psum | solution.py:297
  8.7 8.1 %collective-permute-start = (bf16[3,28,768]{2,1,0:T(8,128)(2,1)S(1)}, bf16[3,28,768]{2,1,0:T(8,128)(2,1)S(1)}, u32[]{:S(2)}, u32[]{:S(2)}) collective-permute-start(bf16[3,28,768]{2,1,0:T(8,128)(2,1)S(1)} %slice.69), channel_id=1, source_target_pairs={{0,24},{8,0},{16,8},{24,16},{1,25},{9,1},{17,9},{25,17},{2,26},{10... | collective-permute-start | bytes 387080 | tf_op jit(solution)/shard_map/ppermute | solution.py:32
  13.5 1.1 copy-start.9
  16.9 5.7 %collective-permute-start.1 = (bf16[28,3,768]{2,1,0:T(4,128)(2,1)S(1)}, bf16[28,3,768]{2,1,0:T(4,128)(2,1)S(1)}, u32[]{:S(2)}, u32[]{:S(2)}) collective-permute-start(bf16[28,3,768]{2,1,0:T(4,128)(2,1)S(1)} %pad_maximum_fusion.3), channel_id=1, source_target_pairs={{0,7},{1,0},{2,1},{3,2},{4,3},{5,4},{6,5},{7,6},{8,15},{9,8},{10,9... | collective-permute-start | bytes 387080 | tf_op jit(solution)/shard_map/ppermute | solution.py:32
  51.7 271.9 %all-reduce.7.cloned.1.call-start = ((), (), s32[]{:S(2)}) async-start(), calls=%async_computation | async-start | bytes 2457600 | tf_op jit(solution)/shard_map/psum | solution.py:340
  51.9 23.3 %copy-start.6 = (bf16[1024,384]{1,0:T(8,128)(2,1)S(1)}, bf16[1024,384]{1,0:T(8,128)(2,1)}, u32[]{:S(2)}) copy-start(bf16[1024,384]{1,0:T(8,128)(2,1)} %get-tuple-element.20) | copy-start | bytes 2359300
  75.3 1.1 copy-start.7
  76.5 2.3 copy-start.8
  76.8 5.3 %collective-permute-start.2 = (bf16[3,28,384]{2,1,0:T(8,128)(2,1)S(1)}, bf16[3,28,384]{2,1,0:T(8,128)(2,1)S(1)}, u32[]{:S(2)}, u32[]{:S(2)}) collective-permute-start(bf16[3,28,384]{2,1,0:T(8,128)(2,1)S(1)} %slice.73), channel_id=1, source_target_pairs={{0,8},{8,16},{16,24},{24,0},{1,9},{9,17},{17,25},{25,1},{2,10},{10... | collective-permute-start | bytes 193544 | tf_op jit(solution)/shard_map/ppermute | solution.py:32
  77.7 5.3 %collective-permute-start.4 = (bf16[3,28,384]{2,1,0:T(8,128)(2,1)S(1)}, bf16[3,28,384]{2,1,0:T(8,128)(2,1)S(1)}, u32[]{:S(2)}, u32[]{:S(2)}) collective-permute-start(bf16[3,28,384]{2,1,0:T(8,128)(2,1)S(1)} %slice.76), channel_id=1, source_target_pairs={{0,8},{8,16},{16,24},{24,0},{1,9},{9,17},{17,25},{25,1},{2,10},{10... | collective-permute-start | bytes 193544 | tf_op jit(solution)/shard_map/ppermute | solution.py:32
  82.2 106.3 %collective-permute-start.3 = (bf16[28,3,384]{2,1,0:T(4,128)(2,1)S(1)}, bf16[28,3,384]{2,1,0:T(4,128)(2,1)S(1)}, u32[]{:S(2)}, u32[]{:S(2)}) collective-permute-start(bf16[28,3,384]{2,1,0:T(4,128)(2,1)S(1)} %pad_maximum_fusion.5), channel_id=1, source_target_pairs={{0,1},{1,2},{2,3},{3,4},{4,5},{5,6},{6,7},{7,0},{8,9},{9,10},{10,1... | collective-permute-start | bytes 193544 | tf_op jit(solution)/shard_map/ppermute | solution.py:32
  83.0 106.6 %collective-permute-start.5 = (bf16[28,3,384]{2,1,0:T(4,128)(2,1)S(1)}, bf16[28,3,384]{2,1,0:T(4,128)(2,1)S(1)}, u32[]{:S(2)}, u32[]{:S(2)}) collective-permute-start(bf16[28,3,384]{2,1,0:T(4,128)(2,1)S(1)} %pad_maximum_fusion.4), channel_id=1, source_target_pairs={{0,1},{1,2},{2,3},{3,4},{4,5},{5,6},{6,7},{7,0},{8,9},{9,10},{10,1... | collective-permute-start | bytes 193544 | tf_op jit(solution)/shard_map/ppermute | solution.py:32
  188.4 2.3 copy-start.3
  189.6 2.3 copy-start.2
  191.9 134.9 %copy-start.4 = (bf16[1536,384]{1,0:T(8,128)(2,1)S(1)}, bf16[1536,384]{1,0:T(8,128)(2,1)}, u32[]{:S(2)}) copy-start(bf16[1536,384]{1,0:T(8,128)(2,1)} %get-tuple-element.32) | copy-start | bytes 3538948
  328.4 1.7 copy-start.1
Sparse Core Ops, SparseCore 0:
  51.8 136.5 all-reduce.8
  193.8 129.7 all-reduce.6
